TPU v7x, 32 devices: a whole 2x2x4 slice. The times are simulated.
32 devices in a mesh: clip: 4 (over x, core), seq: 2 (over y), head: 4 (over z).
Axes of the slice: x: 2, y: 2, z: 4, core: 2. Of those that a mesh axis runs over, the one named last changes fastest.
Arguments:
- inputs: bfloat16 [4, 1500, 768], P('clip', 'seq'), may hold values from -6 to 6
- gain_one: bfloat16 [768], P(('clip', 'seq')), may hold values from 0.25 to 1.75
- shift_one: bfloat16 [768], P(('clip', 'seq')), may hold values from -1.75 to 1.75
- w_query: bfloat16 [768, 768], P(('clip', 'seq'), 'head'), may hold values from -0.21875 to 0.21875
- b_query: bfloat16 [768], P('head'), may hold values from -3 to 3
- w_key: bfloat16 [768, 768], P(('clip', 'seq'), 'head'), may hold values from -0.21875 to 0.21875
- w_value: bfloat16 [768, 768], P(('clip', 'seq'), 'head'), may hold values from -0.21875 to 0.21875
- b_value: bfloat16 [768], P('head'), may hold values from -0.3125 to 0.3125
- w_out: bfloat16 [768, 768], P('head', ('clip', 'seq')), may hold values from -3.5 to 3.5
- b_out: bfloat16 [768], P(('clip', 'seq')), may hold values from -3 to 3
- gain_two: bfloat16 [768], P(('clip', 'seq')), may hold values from 0.25 to 1.75
- shift_two: bfloat16 [768], P(('clip', 'seq')), may hold values from -1.75 to 1.75
- w_fc_one: bfloat16 [768, 3072], P(('clip', 'seq'), 'head'), may hold values from -0.21875 to 0.21875
- b_fc_one: bfloat16 [3072], P('head'), may hold values from -3 to 3
- w_fc_two: bfloat16 [3072, 768], P('head', ('clip', 'seq')), may hold values from -0.3125 to 0.3125
- b_fc_two: bfloat16 [768], P(('clip', 'seq')), may hold values from -3 to 3
- cotangent: bfloat16 [4, 1500, 768], P('clip', 'seq'), may hold values from -6 to 6
Outputs:
- outputs: bfloat16 [4, 1500, 768], P('clip', 'seq')
- input_gradient: float32 [4, 1500, 768], P('clip', 'seq')
- first_gain_gradient: float32 [768], P(('clip', 'seq'))
- grad_shift_one: float32 [768], P(('clip', 'seq'))
- grad_w_query: float32 [768, 768], P(('clip', 'seq'), 'head')
- grad_b_query: float32 [768], P('head')
- grad_w_key: float32 [768, 768], P(('clip', 'seq'), 'head')
- grad_w_value: float32 [768, 768], P(('clip', 'seq'), 'head')
- grad_b_value: float32 [768], P('head')
- grad_w_out: float32 [768, 768], P('head', ('clip', 'seq'))
- grad_b_out: float32 [768], P(('clip', 'seq'))
- second_gain_gradient: float32 [768], P(('clip', 'seq'))
- grad_shift_two: float32 [768], P(('clip', 'seq'))
- grad_w_fc_one: float32 [768, 3072], P(('clip', 'seq'), 'head')
- grad_b_fc_one: float32 [3072], P('head')
- grad_w_fc_two: float32 [3072, 768], P('head', ('clip', 'seq'))
- grad_b_fc_two: float32 [768], P(('clip', 'seq'))
All inputs are finite; a program needn't handle non-finite values.
Results may differ from a plain program's by a relative error of at most 0.012.
Values may be sent and summed in bfloat16 or wider, within the bound.
A program may use at most 128 MiB of HBM per device.

v0:
```python
from functools import partial
import jax
import jax.numpy as jnp
from jax import lax
from jax.sharding import PartitionSpec as P

HEAD_DIM = 64
eps = 1e-05


def layer_norm_forward(values, norm_gain, norm_shift):
    row_mean = jnp.mean(values, axis=-1, keepdims=True)
    centered_values = values - row_mean
    spread = jnp.mean(centered_values * centered_values, axis=-1, keepdims=True)
    inverse_deviation = lax.rsqrt(spread + eps)
    standardized = centered_values * inverse_deviation
    return (standardized * norm_gain + norm_shift, standardized, inverse_deviation)


def layer_norm_backward(output_gradient, standardized, inverse_deviation, norm_gain):
    scaled_rows = output_gradient * norm_gain
    first_row_mean = jnp.mean(scaled_rows, axis=-1, keepdims=True)
    second_row_mean = jnp.mean(scaled_rows * standardized, axis=-1, keepdims=True)
    return inverse_deviation * (scaled_rows - first_row_mean - standardized * second_row_mean)


def fetch_weights(
    gain_one,
    shift_one,
    w_query,
    w_key,
    w_value,
    b_out,
    gain_two,
    shift_two,
    w_fc_one,
    b_fc_two,
    w_out,
    w_fc_two,
):
    rows = (
        lax.all_gather(gain_one, ("clip", "seq"), axis=0, tiled=True),
        lax.all_gather(shift_one, ("clip", "seq"), axis=0, tiled=True),
        lax.all_gather(w_query, ("clip", "seq"), axis=0, tiled=True),
        lax.all_gather(w_key, ("clip", "seq"), axis=0, tiled=True),
        lax.all_gather(w_value, ("clip", "seq"), axis=0, tiled=True),
        lax.all_gather(b_out, ("clip", "seq"), axis=0, tiled=True),
        lax.all_gather(gain_two, ("clip", "seq"), axis=0, tiled=True),
        lax.all_gather(shift_two, ("clip", "seq"), axis=0, tiled=True),
        lax.all_gather(w_fc_one, ("clip", "seq"), axis=0, tiled=True),
        lax.all_gather(b_fc_two, ("clip", "seq"), axis=0, tiled=True),
    )
    columns = (
        lax.all_gather(w_out, ("clip", "seq"), axis=1, tiled=True),
        lax.all_gather(w_fc_two, ("clip", "seq"), axis=1, tiled=True),
    )
    return (rows, columns)


def head_total(partial_sum):
    return lax.psum(partial_sum, "head")


def on_device(
    inputs,
    gain_one,
    shift_one,
    w_query,
    b_query,
    w_key,
    w_value,
    b_value,
    w_out,
    b_out,
    gain_two,
    shift_two,
    w_fc_one,
    b_fc_one,
    w_fc_two,
    b_fc_two,
    cotangent,
):
    clips, frames, width = inputs.shape
    local = w_query.shape[1]
    heads = local // HEAD_DIM
    scale = HEAD_DIM ** (-0.5)
    gathered_rows = jnp.float32
    count = clips * frames
    rows, columns = fetch_weights(
        gain_one,
        shift_one,
        w_query,
        w_key,
        w_value,
        b_out,
        gain_two,
        shift_two,
        w_fc_one,
        b_fc_two,
        w_out,
        w_fc_two,
    )
    (
        full_gain_one,
        gathered_first_shift,
        full_query,
        full_key,
        full_value,
        full_b_out,
        full_gain_two,
        gathered_second_shift,
        full_fc_one,
        full_b_fc_two,
    ) = rows
    full_out, full_fc_two = columns
    token_rows = inputs.astype(gathered_rows).reshape(count, width)
    first_norm_gain = full_gain_one.astype(gathered_rows)
    second_norm_gain = full_gain_two.astype(gathered_rows)
    normalized_gathered, first_standardized, first_inverse_deviation = layer_norm_forward(
        token_rows, first_norm_gain, gathered_first_shift.astype(gathered_rows)
    )
    normed_one = normalized_gathered.astype(jnp.bfloat16)
    query = (
        jnp.dot(normed_one, full_query, preferred_element_type=gathered_rows)
        + b_query.astype(gathered_rows)
    ).astype(jnp.bfloat16)
    key = jnp.dot(normed_one, full_key, preferred_element_type=gathered_rows).astype(jnp.bfloat16)
    value = (
        jnp.dot(normed_one, full_value, preferred_element_type=gathered_rows)
        + b_value.astype(gathered_rows)
    ).astype(jnp.bfloat16)
    query_clips = query.reshape(clips, frames, local)
    key_all, value_all = (
        lax.all_gather(key.reshape(clips, frames, local), "seq", axis=1, tiled=True),
        lax.all_gather(value.reshape(clips, frames, local), "seq", axis=1, tiled=True),
    )

    def attend(block):
        query_block, key_block, value_block = block
        query_heads = query_block.reshape(frames, heads, HEAD_DIM)
        key_heads = key_block.reshape(-1, heads, HEAD_DIM)
        value_heads = value_block.reshape(-1, heads, HEAD_DIM)
        scores = (
            jnp.einsum("qhd,khd->hqk", query_heads, key_heads, preferred_element_type=gathered_rows)
            * scale
        )
        top = jnp.max(scores, axis=-1, keepdims=True)
        expo = jnp.exp(scores - top)
        total = jnp.sum(expo, axis=-1, keepdims=True)
        probs = (expo / total).astype(jnp.bfloat16)
        result = jnp.einsum(
            "hqk,khd->qhd", probs, value_heads, preferred_element_type=gathered_rows
        )
        return (result.reshape(frames, local).astype(jnp.bfloat16), (top + jnp.log(total))[..., 0])

    attended_clips, log_totals = lax.map(attend, (query_clips, key_all, value_all))
    attended = attended_clips.reshape(count, local)
    attn_terms = jnp.dot(attended, full_out, preferred_element_type=gathered_rows)
    middle_state = token_rows + head_total(attn_terms) + full_b_out.astype(gathered_rows)
    normalized_middle, second_standardized, second_inverse_deviation = layer_norm_forward(
        middle_state, second_norm_gain, gathered_second_shift.astype(gathered_rows)
    )
    normed_two = normalized_middle.astype(jnp.bfloat16)
    pre = jnp.dot(normed_two, full_fc_one, preferred_element_type=gathered_rows) + b_fc_one.astype(
        gathered_rows
    )
    act = jax.nn.gelu(pre, approximate=False).astype(jnp.bfloat16)
    ffn_terms = jnp.dot(act, full_fc_two, preferred_element_type=gathered_rows)
    outputs = (middle_state + head_total(ffn_terms) + full_b_fc_two.astype(gathered_rows)).astype(
        jnp.bfloat16
    )
    rows, columns = fetch_weights(
        gain_one,
        shift_one,
        w_query,
        w_key,
        w_value,
        b_out,
        gain_two,
        shift_two,
        w_fc_one,
        b_fc_two,
        w_out,
        w_fc_two,
    )
    (
        full_gain_one,
        gathered_first_shift,
        full_query,
        full_key,
        full_value,
        full_b_out,
        full_gain_two,
        gathered_second_shift,
        full_fc_one,
        full_b_fc_two,
    ) = rows
    full_out, full_fc_two = columns
    first_norm_gain = full_gain_one.astype(gathered_rows)
    second_norm_gain = full_gain_two.astype(gathered_rows)
    upstream_gradient = cotangent.astype(gathered_rows).reshape(count, width)
    grad_b_fc_two = jnp.sum(upstream_gradient, axis=0)
    grad_top_low = upstream_gradient.astype(jnp.bfloat16)
    grad_w_fc_two = jnp.einsum("tf,td->fd", act, grad_top_low, preferred_element_type=gathered_rows)
    grad_act = jnp.einsum(
        "td,fd->tf", grad_top_low, full_fc_two, preferred_element_type=gathered_rows
    )
    unused, gelu_back = jax.vjp(partial(jax.nn.gelu, approximate=False), pre)
    grad_pre = gelu_back(grad_act)[0].astype(jnp.bfloat16)
    grad_b_fc_one = jnp.sum(grad_pre.astype(gathered_rows), axis=0)
    grad_w_fc_one = jnp.einsum(
        "td,tf->df", normed_two, grad_pre, preferred_element_type=gathered_rows
    )
    normed_two_terms = jnp.einsum(
        "tf,df->td", grad_pre, full_fc_one, preferred_element_type=gathered_rows
    )
    second_normalized_gradient = head_total(normed_two_terms)
    middle_gradient = upstream_gradient + layer_norm_backward(
        second_normalized_gradient, second_standardized, second_inverse_deviation, second_norm_gain
    )
    grad_mid_low = middle_gradient.astype(jnp.bfloat16)
    second_gain_gradient = jnp.sum(second_normalized_gradient * second_standardized, axis=0)
    grad_shift_two = jnp.sum(second_normalized_gradient, axis=0)
    grad_b_out = jnp.sum(middle_gradient, axis=0)
    grad_w_out = jnp.einsum(
        "tj,td->jd", attended, grad_mid_low, preferred_element_type=gathered_rows
    )
    grad_attended = jnp.einsum(
        "td,jd->tj", grad_mid_low, full_out, preferred_element_type=gathered_rows
    ).astype(jnp.bfloat16)

    def attend_back(block):
        query_block, key_block, value_block, grad_block, log_block = block
        query_heads = query_block.reshape(frames, heads, HEAD_DIM)
        key_heads = key_block.reshape(-1, heads, HEAD_DIM)
        value_heads = value_block.reshape(-1, heads, HEAD_DIM)
        grad_heads = grad_block.reshape(frames, heads, HEAD_DIM)
        scores = (
            jnp.einsum("qhd,khd->hqk", query_heads, key_heads, preferred_element_type=gathered_rows)
            * scale
        )
        probs = jnp.exp(scores - log_block[..., None])
        grad_values = jnp.einsum(
            "hqk,qhd->khd",
            probs.astype(jnp.bfloat16),
            grad_heads,
            preferred_element_type=gathered_rows,
        )
        grad_probs = jnp.einsum(
            "qhd,khd->hqk", grad_heads, value_heads, preferred_element_type=gathered_rows
        )
        inner = jnp.sum(probs * grad_probs, axis=-1, keepdims=True)
        grad_scores = (probs * (grad_probs - inner)).astype(jnp.bfloat16)
        grad_queries = (
            jnp.einsum("hqk,khd->qhd", grad_scores, key_heads, preferred_element_type=gathered_rows)
            * scale
        )
        grad_keys = (
            jnp.einsum(
                "hqk,qhd->khd", grad_scores, query_heads, preferred_element_type=gathered_rows
            )
            * scale
        )
        return (
            grad_queries.reshape(frames, local).astype(jnp.bfloat16),
            grad_keys.reshape(-1, local),
            grad_values.reshape(-1, local),
        )

    grad_query_clips, grad_key_all, grad_value_all = lax.map(
        attend_back,
        (query_clips, key_all, value_all, grad_attended.reshape(clips, frames, local), log_totals),
    )
    grad_key_own, grad_value_own = (
        lax.psum_scatter(grad_key_all, "seq", scatter_dimension=1, tiled=True),
        lax.psum_scatter(grad_value_all, "seq", scatter_dimension=1, tiled=True),
    )
    grad_query = grad_query_clips.reshape(count, local)
    grad_key = grad_key_own.reshape(count, local).astype(jnp.bfloat16)
    grad_value = grad_value_own.reshape(count, local).astype(jnp.bfloat16)
    grad_b_query = jnp.sum(grad_query.astype(gathered_rows), axis=0)
    grad_b_value = jnp.sum(grad_value.astype(gathered_rows), axis=0)
    grad_w_query = jnp.einsum(
        "td,tj->dj", normed_one, grad_query, preferred_element_type=gathered_rows
    )
    grad_w_key = jnp.einsum("td,tj->dj", normed_one, grad_key, preferred_element_type=gathered_rows)
    grad_w_value = jnp.einsum(
        "td,tj->dj", normed_one, grad_value, preferred_element_type=gathered_rows
    )
    grad_normed_part = jnp.einsum(
        "tj,dj->td", grad_query, full_query, preferred_element_type=gathered_rows
    )
    grad_normed_part = grad_normed_part + jnp.einsum(
        "tj,dj->td", grad_key, full_key, preferred_element_type=gathered_rows
    )
    grad_normed_part = grad_normed_part + jnp.einsum(
        "tj,dj->td", grad_value, full_value, preferred_element_type=gathered_rows
    )
    first_normalized_gradient = head_total(grad_normed_part)
    first_gain_gradient = jnp.sum(first_normalized_gradient * first_standardized, axis=0)
    grad_shift_one = jnp.sum(first_normalized_gradient, axis=0)
    input_gradient = middle_gradient + layer_norm_backward(
        first_normalized_gradient, first_standardized, first_inverse_deviation, first_norm_gain
    )
    owned_rows = (
        lax.psum_scatter(first_gain_gradient, ("clip", "seq"), scatter_dimension=0, tiled=True),
        lax.psum_scatter(grad_shift_one, ("clip", "seq"), scatter_dimension=0, tiled=True),
        lax.psum_scatter(grad_w_query, ("clip", "seq"), scatter_dimension=0, tiled=True),
        lax.psum_scatter(grad_w_key, ("clip", "seq"), scatter_dimension=0, tiled=True),
        lax.psum_scatter(grad_w_value, ("clip", "seq"), scatter_dimension=0, tiled=True),
        lax.psum_scatter(grad_b_out, ("clip", "seq"), scatter_dimension=0, tiled=True),
        lax.psum_scatter(second_gain_gradient, ("clip", "seq"), scatter_dimension=0, tiled=True),
        lax.psum_scatter(grad_shift_two, ("clip", "seq"), scatter_dimension=0, tiled=True),
        lax.psum_scatter(grad_w_fc_one, ("clip", "seq"), scatter_dimension=0, tiled=True),
        lax.psum_scatter(grad_b_fc_two, ("clip", "seq"), scatter_dimension=0, tiled=True),
    )
    owned_columns = (
        lax.psum_scatter(grad_w_out, ("clip", "seq"), scatter_dimension=1, tiled=True),
        lax.psum_scatter(grad_w_fc_two, ("clip", "seq"), scatter_dimension=1, tiled=True),
    )
    bias_totals = lax.psum((grad_b_query, grad_b_value, grad_b_fc_one), ("clip", "seq"))
    return (
        outputs.reshape(clips, frames, width),
        input_gradient.reshape(clips, frames, width),
        owned_rows[0],
        owned_rows[1],
        owned_rows[2],
        bias_totals[0],
        owned_rows[3],
        owned_rows[4],
        bias_totals[1],
        owned_columns[0],
        owned_rows[5],
        owned_rows[6],
        owned_rows[7],
        owned_rows[8],
        bias_totals[2],
        owned_columns[1],
        owned_rows[9],
    )


def solution(mesh):
    return jax.shard_map(
        on_device,
        mesh=mesh,
        in_specs=(
            P("clip", "seq", None),
            P(("clip", "seq")),
            P(("clip", "seq")),
            P(("clip", "seq"), "head"),
            P("head"),
            P(("clip", "seq"), "head"),
            P(("clip", "seq"), "head"),
            P("head"),
            P("head", ("clip", "seq")),
            P(("clip", "seq")),
            P(("clip", "seq")),
            P(("clip", "seq")),
            P(("clip", "seq"), "head"),
            P("head"),
            P("head", ("clip", "seq")),
            P(("clip", "seq")),
            P("clip", "seq", None),
        ),
        out_specs=(
            P("clip", "seq", None),
            P("clip", "seq", None),
            P(("clip", "seq")),
            P(("clip", "seq")),
            P(("clip", "seq"), "head"),
            P("head"),
            P(("clip", "seq"), "head"),
            P(("clip", "seq"), "head"),
            P("head"),
            P("head", ("clip", "seq")),
            P(("clip", "seq")),
            P(("clip", "seq")),
            P(("clip", "seq")),
            P(("clip", "seq"), "head"),
            P("head"),
            P("head", ("clip", "seq")),
            P(("clip", "seq")),
        ),
        check_vma=False,
    )
```

profile of v0, /device:TPU:0, one launch (start us, length us, event | category | flops | bytes accessed | tf_op | source)
XLA Modules:
  0.0 687.4 jit_solution(10025798544051608802)
XLA Ops:
  15.1 25.7 %all-reduce.17 = (bf16[768]{0:T(1024)(128)(2,1)S(1)}, bf16[768]{0:T(1024)(128)(2,1)S(1)}, bf16[768]{0:T(1024)(128)(2,1)S(1)}, bf16[768]{0:T(1024)(128)(2,1)S(1)}...) all-reduce(bf16[768]{0:T(1024)(128)(2,1)S(1)} %dynamic-update-slice, ...), channel_id=1, replica_groups=mesh['clip'=4,'seq'=2,'head'=4] {'clip','seq'}, use_global_device_ids=true, to_apply=%add.1 | all-reduce | flops 4608 | bytes 18432
  44.1 15.9 %all_gather.55 = bf16[768,192]{1,0:T(8,128)(2,1)S(1)} all-gather(bf16[96,192]{1,0:T(8,128)(2,1)S(1)} %copy-done.26), channel_id=1, replica_groups=mesh['clip'=4,'seq'=2,'head'=4] {'clip','seq'}, dimensions={0}, use_global_device_ids=true | all-gather | bytes 331776 | tf_op jit(solution)/shard_map/all_gather | solution.py:45
  61.1 10.5 %all-gather.3 = bf16[2,750,192]{1,2,0:T(8,128)(2,1)S(1)} all-gather(bf16[1,750,192]{1,2,0:T(8,128)(2,1)S(1)} %fusion.39), channel_id=3, replica_groups=mesh['clip'=4,'seq'=2,'head'=4] {'seq'}, dimensions={0}, use_global_device_ids=true | all-gather | bytes 864000 | tf_op jit(solution)/shard_map/all_gather | solution.py:134
  75.3 15.6 %all_gather.54 = bf16[768,192]{1,0:T(8,128)(2,1)S(1)} all-gather(bf16[96,192]{1,0:T(8,128)(2,1)S(1)} %copy-done.27), channel_id=1, replica_groups=mesh['clip'=4,'seq'=2,'head'=4] {'clip','seq'}, dimensions={0}, use_global_device_ids=true | all-gather | bytes 331776 | tf_op jit(solution)/shard_map/all_gather | solution.py:44
  91.0 16.6 %all_gather.52 = bf16[768,192]{1,0:T(8,128)(2,1)S(1)} all-gather(bf16[96,192]{1,0:T(8,128)(2,1)S(1)} %copy-done.28), channel_id=1, replica_groups=mesh['clip'=4,'seq'=2,'head'=4] {'clip','seq'}, dimensions={0}, use_global_device_ids=true | all-gather | bytes 331776 | tf_op jit(solution)/shard_map/all_gather | solution.py:46
  108.9 9.9 %all-gather.2 = bf16[2,750,192]{1,2,0:T(8,128)(2,1)S(1)} all-gather(bf16[1,750,192]{1,2,0:T(8,128)(2,1)S(1)} %fusion.40), channel_id=2, replica_groups=mesh['clip'=4,'seq'=2,'head'=4] {'seq'}, dimensions={0}, use_global_device_ids=true | all-gather | bytes 864000 | tf_op jit(solution)/shard_map/all_gather | solution.py:135
  120.2 2.9 reshape.250
  123.2 16.6 %all_gather.57 = bf16[192,768]{0,1:T(8,128)(2,1)S(1)} all-gather(bf16[192,96]{0,1:T(8,128)(2,1)S(1)} %copy.40), channel_id=1, replica_groups=mesh['clip'=4,'seq'=2,'head'=4] {'clip','seq'}, dimensions={1}, use_global_device_ids=true | all-gather | bytes 331776 | tf_op jit(solution)/shard_map/all_gather | solution.py:54
  140.4 7.0 %multiply_reduce_fusion.1 = (f32[3,750]{1,0:T(4,128)S(1)}, f32[3,750,1500]{2,1,0:T(8,128)}) fusion(bf16[750,3,64]{0,2,1:T(8,128)(2,1)S(1)} %bitcast.146, bf16[1500,3,64]{0,2,1:T(8,128)(2,1)S(1)} %reshape.253), kind=kOutput, calls=%fused_computation.6 | convolution fusion | flops 438747744 | bytes 14373000 | tf_op jit(solution)/shard_map/while/body/eval_jaxpr/qhd,khd->hqk/dot_general | solution.py:144
  147.4 7.4 %fusion = f32[3,750]{1,0:T(4,128)S(1)} fusion(f32[3,750,1500]{2,1,0:T(8,128)} %get-tuple-element.151, f32[3,750]{1,0:T(4,128)S(1)} %get-tuple-element.150), kind=kLoop, calls=%fused_computation.5 | loop fusion | flops 10122750 | bytes 13518000 | tf_op jit(solution)/shard_map/while/body/eval_jaxpr/reduce_sum | solution.py:149
  154.8 6.6 fusion.38
  164.7 94.1 %all-reduce.23.cloned.1.call-done = f32[750,768]{1,0:T(8,128)} async-done(((f32[750,768]{1,0:T(8,128)}), f32[750,768]{1,0:T(8,128)}) %all-reduce.23.cloned.1.call-update) | async-done | bytes 2304016 | tf_op jit(solution)/shard_map/psum | solution.py:61
  261.2 8.9 %multiply_convert_fusion.1 = (bf16[750,768]{1,0:T(8,128)(2,1)}, f32[750,768]{1,0:T(8,128)}, f32[750,768]{1,0:T(8,128)}) fusion(f32[768]{0:T(1024)S(1)} %convert_element_type.151, bf16[768,768]{1,0:T(8,128)(2,1)} %all-gather.7.cloned.1.call-done, f32[750,768]{1,0:T(8,128)S(1)} %get-tuple-element.147, f32[768]{0:T(1024)S(1)} %convert_element_type.149, ...), kind=kOutput, calls=%fused_computation.48 | convolution fusion | flops 925632000 | bytes 9258864 | tf_op jit(solution)/shard_map/dot_general | solution.py:164
  270.1 4.8 convert_reduce_fusion.2
  275.9 2.5 fusion.72
  280.3 4.1 fusion.71
  284.4 86.5 %all-reduce.25.cloned.1.call-done = f32[750,768]{1,0:T(8,128)} async-done(((f32[750,768]{1,0:T(8,128)}), f32[750,768]{1,0:T(8,128)}) %all-reduce.25.cloned.1.call-update) | async-done | bytes 2304016 | tf_op jit(solution)/shard_map/psum | solution.py:61
  370.9 2.9 multiply_reduce_fusion.2
  376.9 7.7 %fusion.2 = f32[3,64,1500]{2,1,0:T(8,128)} fusion(bf16[750,3,64]{0,2,1:T(8,128)(2,1)S(1)} %bitcast.144, f32[3,750,1500]{2,1,0:T(8,128)} %get-tuple-element.151, f32[3,750]{1,0:T(4,128)S(1)} %log_add_fusion), kind=kOutput, calls=%fused_computation.8 | convolution fusion | flops 442124992 | bytes 14949000 | tf_op jit(solution)/shard_map/while/body/eval_jaxpr/hqk,qhd->khd/dot_general | solution.py:243
  384.6 7.0 %multiply_reduce_fusion = (f32[3,750]{1,0:T(4,128)S(1)}, f32[3,750,1500]{2,1,0:T(8,128)}) fusion(f32[3,750,1500]{2,1,0:T(8,128)S(1)} %bitcast.141, f32[3,750]{1,0:T(4,128)S(1)} %log_add_fusion, bf16[750,3,64]{0,2,1:T(8,128)(2,1)S(1)} %bitcast.145, bf16[1500,3,64]{0,2,1:T(8,128)(2,1)S(1)} %copy-done.18), kind=kOutput, calls=%fused_computation.1 | convolution fusion | flops 445497760 | bytes 27882000 | tf_op jit(solution)/shard_map/while/body/eval_jaxpr/qhd,khd->hqk/dot_general | solution.py:249
  391.6 6.9 multiply_convert_fusion
  400.9 2.8 convert_reduce_fusion.4
  405.2 62.3 %all-reduce.28 = (bf16[1,1500,192]{1,2,0:T(8,128)(2,1)}, bf16[1,1500,192]{1,2,0:T(8,128)(2,1)}) all-reduce(f32[1,1500,192]{1,2,0:T(8,128)} %bitcast.142, f32[1,1500,192]{1,2,0:T(8,128)} %bitcast.143), channel_id=4, replica_groups=mesh['clip'=4,'seq'=2,'head'=4] {'seq'}, use_global_device_ids=true, to_apply=%region_12.13.clone | all-reduce | flops 576000 | bytes 3456000
  475.7 3.3 fusion.53
  479.1 2.7 fusion.74
  481.9 4.2 fusion.61
  486.1 4.2 fusion.43
  494.2 145.7 %all-reduce.27.cloned.1.call-done = (f32[750,768]{1,0:T(8,128)}, f32[750,768]{1,0:T(8,128)}) async-done(((f32[750,768]{1,0:T(8,128)}, f32[750,768]{1,0:T(8,128)}), (f32[750,768]{1,0:T(8,128)}, f32[750,768]{1,0:T(8,128)})) %all-reduce.27.cloned.1.call-update) | async-done | bytes 4608016 | tf_op jit(solution)/shard_map/psum | solution.py:61
  639.9 2.7 fusion.22
  642.5 25.1 %all-reduce.14 = (f32[768]{0:T(1024)S(1)}, f32[768]{0:T(1024)S(1)}, f32[192]{0:T(256)}, f32[192]{0:T(256)}, f32[768]{0:T(1024)S(1)}, /*index=5*/f32[768]{0:T(102...) all-reduce(f32[768]{0:T(1024)S(1)} %get-tuple-element.115, ...), channel_id=6, replica_groups=mesh['clip'=4,'seq'=2,'head'=4] {'clip','seq'}, use_global_device_ids=true, to_apply=%region_18.19.clone | all-reduce | flops 5760 | bytes 46080
  671.1 2.8 fusion.21
  673.9 3.8 copy.41
  (175 shorter events, 49.8 us)
Async XLA Ops:
  8.0 52.0 %copy-start = (bf16[1,750,768]{2,1,0:T(8,128)(2,1)S(1)}, bf16[1,750,768]{2,1,0:T(8,128)(2,1)}, u32[]{:S(2)}) copy-start(bf16[1,750,768]{2,1,0:T(8,128)(2,1)} %param.17) | copy-start | bytes 3456004
  8.0 36.0 %copy-start.26 = (bf16[96,192]{1,0:T(8,128)(2,1)S(1)}, bf16[96,192]{1,0:T(8,128)(2,1)}, u32[]{:S(2)}) copy-start(bf16[96,192]{1,0:T(8,128)(2,1)} %param.22) | copy-start | bytes 110596
  8.0 250.7 %all-reduce.23.cloned.1.call-start = ((), (), s32[]{:S(2)}) async-start(), calls=%async_computation.6 | async-start | bytes 4620288 | tf_op jit(solution)/shard_map/psum | solution.py:61
  60.0 11.6 %copy-start.8 = (bf16[768,192]{1,0:T(8,128)(2,1)}, bf16[768,192]{1,0:T(8,128)(2,1)S(1)}, u32[]{:S(2)}) copy-start(bf16[768,192]{1,0:T(8,128)(2,1)S(1)} %all_gather.55) | copy-start | bytes 884740
  60.5 14.8 %copy-start.27 = (bf16[96,192]{1,0:T(8,128)(2,1)S(1)}, bf16[96,192]{1,0:T(8,128)(2,1)}, u32[]{:S(2)}) copy-start(bf16[96,192]{1,0:T(8,128)(2,1)} %param.20) | copy-start | bytes 110596
  60.5 30.5 %copy-start.32 = (bf16[192]{0:T(256)(128)(2,1)S(1)}, bf16[192]{0:T(256)(128)(2,1)}, u32[]{:S(2)}) copy-start(bf16[192]{0:T(256)(128)(2,1)} %param.21) | copy-start | bytes 1156
  60.5 30.5 %copy-start.28 = (bf16[96,192]{1,0:T(8,128)(2,1)S(1)}, bf16[96,192]{1,0:T(8,128)(2,1)}, u32[]{:S(2)}) copy-start(bf16[96,192]{1,0:T(8,128)(2,1)} %param.23) | copy-start | bytes 110596
  61.1 46.5 %copy-start.33 = (bf16[192]{0:T(256)(128)(2,1)S(1)}, bf16[192]{0:T(256)(128)(2,1)}, u32[]{:S(2)}) copy-start(bf16[192]{0:T(256)(128)(2,1)} %param.24) | copy-start | bytes 1156
  75.3 65.1 %copy-start.5 = (bf16[1500,3,64]{0,2,1:T(8,128)(2,1)}, bf16[1500,3,64]{0,2,1:T(8,128)(2,1)S(1)}, u32[]{:S(2)}) copy-start(bf16[1500,3,64]{0,2,1:T(8,128)(2,1)S(1)} %reshape.253) | copy-start | bytes 1728004
  91.0 48.8 %copy-start.9 = (bf16[768,192]{1,0:T(8,128)(2,1)}, bf16[768,192]{1,0:T(8,128)(2,1)S(1)}, u32[]{:S(2)}) copy-start(bf16[768,192]{1,0:T(8,128)(2,1)S(1)} %all_gather.54) | copy-start | bytes 884740
  108.4 14.7 %copy-start.29 = (bf16[192,96]{1,0:T(8,128)(2,1)S(1)}, bf16[192,96]{1,0:T(8,128)(2,1)}, u32[]{:S(2)}) copy-start(bf16[192,96]{1,0:T(8,128)(2,1)} %param.25) | copy-start | bytes 110596
  139.8 21.6 %copy-start.11 = (bf16[192,768]{0,1:T(8,128)(2,1)}, bf16[192,768]{0,1:T(8,128)(2,1)S(1)}, u32[]{:S(2)}) copy-start(bf16[192,768]{0,1:T(8,128)(2,1)S(1)} %all_gather.57) | copy-start | bytes 884740
  140.4 7.0 %copy-start.15 = (bf16[750,192]{0,1:T(8,128)(2,1)}, bf16[750,192]{0,1:T(8,128)(2,1)S(1)}, u32[]{:S(2)}) copy-start(bf16[750,192]{0,1:T(8,128)(2,1)S(1)} %fusion.36) | copy-start | bytes 864004
  147.4 7.4 %copy-start.17 = (bf16[1500,3,64]{0,2,1:T(8,128)(2,1)S(1)}, bf16[1500,3,64]{0,2,1:T(8,128)(2,1)}, u32[]{:S(2)}) copy-start(bf16[1500,3,64]{0,2,1:T(8,128)(2,1)} %reshape.250) | copy-start | bytes 1728004
  163.4 97.8 %all-gather.7.cloned.1.call-start = ((), (), s32[]{:S(2)}) async-start(), calls=%async_computation.7 | async-start | bytes 1327104 | tf_op jit(solution)/shard_map/all_gather | solution.py:50
  164.0 106.1 %all-gather.9.cloned.1.call-start = ((), (), s32[]{:S(2)}) async-start(), calls=%async_computation.8 | async-start | bytes 1327104 | tf_op jit(solution)/shard_map/all_gather | solution.py:55
  164.6 206.4 %all-reduce.25.cloned.1.call-start = ((), (), s32[]{:S(2)}) async-start(), calls=%async_computation.9 | async-start | bytes 4620288 | tf_op jit(solution)/shard_map/psum | solution.py:61
  270.1 5.8 copy-start.31
  278.4 214.1 %reduce-scatter.21.cloned.1.call-start = ((), (), s32[]{:S(2)}) async-start(), calls=%async_computation.15 | async-start | bytes 884736
  370.9 5.4 copy-start.12
  373.8 10.8 %slice-start = ((s8[13860864]{0:T(1024)(128)(4,1)}), s8[4194304]{0:T(1024)(128)(4,1)S(1)}, s32[]{:S(2)}) async-start(s8[13860864]{0:T(1024)(128)(4,1)} %bitcast.140), calls=%async_computation.17 | async-start | bytes 8388608
  373.8 10.8 %slice-start.1 = ((s8[13860864]{0:T(1024)(128)(4,1)}), s8[4194304]{0:T(1024)(128)(4,1)S(1)}, s32[]{:S(2)}) async-start(s8[13860864]{0:T(1024)(128)(4,1)} %bitcast.140), calls=%async_computation.18 | async-start | bytes 8388608
  376.9 7.7 %slice-start.2 = ((s8[13860864]{0:T(1024)(128)(4,1)}), s8[4194304]{0:T(1024)(128)(4,1)S(1)}, s32[]{:S(2)}) async-start(s8[13860864]{0:T(1024)(128)(4,1)} %bitcast.140), calls=%async_computation.19 | async-start | bytes 8388608
  376.9 7.7 %slice-start.3 = ((s8[13860864]{0:T(1024)(128)(4,1)}), s8[1277952]{0:T(1024)(128)(4,1)S(1)}, s32[]{:S(2)}) async-start(s8[13860864]{0:T(1024)(128)(4,1)} %bitcast.140), calls=%async_computation.20 | async-start | bytes 2555904
  376.9 7.7 %copy-start.18 = (bf16[1500,3,64]{0,2,1:T(8,128)(2,1)S(1)}, bf16[1500,3,64]{0,2,1:T(8,128)(2,1)}, u32[]{:S(2)}) copy-start(bf16[1500,3,64]{0,2,1:T(8,128)(2,1)} %reshape.250) | copy-start | bytes 1728004
  391.6 6.9 %copy-start.16 = (bf16[750,192]{0,1:T(8,128)(2,1)S(1)}, bf16[750,192]{0,1:T(8,128)(2,1)}, u32[]{:S(2)}) copy-start(bf16[750,192]{0,1:T(8,128)(2,1)} %copy-done.15) | copy-start | bytes 864004
  405.2 234.7 %all-reduce.27.cloned.1.call-start = ((), (), s32[]{:S(2)}) async-start(), calls=%async_computation.16 | async-start | bytes 9240576 | tf_op jit(solution)/shard_map/psum | solution.py:61
  472.4 206.7 %reduce-scatter.15.cloned.1.call-start = ((), (), s32[]{:S(2)}) async-start(), calls=%async_computation.12 | async-start | bytes 884736 | tf_op jit(solution)/shard_map/reduce_scatter | solution.py:310
  475.6 203.5 %reduce-scatter.13.cloned.1.call-start = ((), (), s32[]{:S(2)}) async-start(), calls=%async_computation.11 | async-start | bytes 884736 | tf_op jit(solution)/shard_map/reduce_scatter | solution.py:309
  479.0 200.0 %reduce-scatter.11.cloned.1.call-start = ((), (), s32[]{:S(2)}) async-start(), calls=%async_computation.10 | async-start | bytes 884736 | tf_op jit(solution)/shard_map/reduce_scatter | solution.py:308
  481.8 197.3 %reduce-scatter.17.cloned.1.call-start = ((), (), s32[]{:S(2)}) async-start(), calls=%async_computation.13 | async-start | bytes 2654208 | tf_op jit(solution)/shard_map/reduce_scatter | solution.py:314
  486.1 194.0 %reduce-scatter.19.cloned.1.call-start = ((), (), s32[]{:S(2)}) async-start(), calls=%async_computation.14 | async-start | bytes 2654208 | tf_op jit(solution)/shard_map/reduce_scatter | solution.py:319
  (19 other events, 37.1 us)
Sparse Core Ops, SparseCore 0:
  163.5 95.1 all-reduce.22
  278.5 92.3 all-reduce.24
  472.5 167.2 all-reduce.26
Sparse Core Ops, SparseCore 1:
  165.8 25.6 all-gather.6
  193.2 23.8 all-gather.8
  405.3 36.4 reduce-scatter.20
  476.9 33.4 reduce-scatter.14
  514.1 34.9 reduce-scatter.12
  552.8 34.9 reduce-scatter.10
  591.5 42.2 reduce-scatter.16
  637.6 42.4 reduce-scatter.18
where the time goes:
time: 695 us; the launch traced here: 687 us
  waiting for transfers between devices  328 us (47%)
  blocking collectives  198 us (28%)
  matrix products  79.4 us (11%)
  other arithmetic  33.5 us (5%)
  local copies, waits for them, and re-layouts  28.8 us (4%)
  between operations  18.1 us (3%)
    psum x3, waiting for transfers between devices, head_total(): return lax.psum(partial_sum, 'head')  326 us
    unnamed x3, blocking collectives  113 us
    unnamed x103, local copies, waits for them, and re-layouts  20.8 us
    all_gather x1, blocking collectives, fetch_weights(): lax.all_gather(w_value, ('clip', 'seq'), axis=0, tiled=True)  16.6 us
    all_gather x1, blocking collectives, fetch_weights(): lax.all_gather(w_out, ('clip', 'seq'), axis=1, tiled=True)  16.6 us
    all_gather x1, blocking collectives, fetch_weights(): lax.all_gather(w_key, ('clip', 'seq'), axis=0, tiled=True)  15.9 us
    all_gather x1, blocking collectives, fetch_weights(): lax.all_gather(w_query, ('clip', 'seq'), axis=0, tiled=True)  15.6 us
  transfers between devices with their start and end apart: 11, of which 4 were waited for; matrix products, arithmetic and copies ran while one was open for 8% of the time, Pallas kernels for 0%

commit v1 on v0

--- a/solution.py
+++ b/solution.py
@@ -1,11 +1,30 @@
+import functools
 from functools import partial
 import jax
 import jax.numpy as jnp
 from jax import lax
 from jax.sharding import PartitionSpec as P
+from jax.lax import axis_index, axis_size, ppermute
 
 HEAD_DIM = 64
 eps = 1e-05
+
+
+def move_lots_all_now(packet, mesh_name, at_axis):
+    prior, view_out = (axis_size(mesh_name), axis_index(mesh_name))
+    tile_out, f_next = (packet, 1)
+    while f_next < prior:
+        row_out = ppermute(
+            tile_out, axis_name=mesh_name, perm=[(c, c ^ f_next) for c in range(prior)]
+        )
+        e_now = jnp.concatenate([tile_out, row_out], axis=at_axis)
+        val2 = jnp.concatenate([row_out, tile_out], axis=at_axis)
+        tile_out = jnp.where(view_out & f_next == 0, e_now, val2)
+        f_next = 2 * f_next
+    return tile_out
+
+
+pack_corner = functools.partial(move_lots_all_now, mesh_name=("clip", "seq"), at_axis=0)
 
 
 def layer_norm_forward(values, norm_gain, norm_shift):
@@ -41,7 +60,7 @@
     rows = (
         lax.all_gather(gain_one, ("clip", "seq"), axis=0, tiled=True),
         lax.all_gather(shift_one, ("clip", "seq"), axis=0, tiled=True),
-        lax.all_gather(w_query, ("clip", "seq"), axis=0, tiled=True),
+        pack_corner(w_query),
         lax.all_gather(w_key, ("clip", "seq"), axis=0, tiled=True),
         lax.all_gather(w_value, ("clip", "seq"), axis=0, tiled=True),
         lax.all_gather(b_out, ("clip", "seq"), axis=0, tiled=True),

time: 695 us -> 716 us (1.030)
  waiting for transfers between devices: 328 us -> 352 us
  blocking collectives: 198 us -> 175 us
  matrix products: 79.4 us -> 90.1 us
    reduce_scatter x1, waiting for transfers between devices: 0.97 us -> 26 us  [on_device(): lax.psum_scatter(grad_w_fc_two, ('clip', 'seq'), scatter_dimension=1, til...]
    all_gather x1 -> x0, blocking collectives: 15.6 us -> none  [fetch_weights(): lax.all_gather(w_query, ('clip', 'seq'), axis=0, tiled=True)]
  transfers between devices with their start and end apart: 11 -> 14, of which waited for: 4 -> 5; matrix products, arithmetic and copies ran while one was open for 8% -> 11% of each run, Pallas kernels for 0% -> 0%
where the time goes in v1:
time: 716 us; the launch traced here: 709 us
  waiting for transfers between devices  352 us (49%)
  blocking collectives  175 us (24%)
  matrix products  90.1 us (13%)
  other arithmetic  37.9 us (5%)
  local copies, waits for them, and re-layouts  30.3 us (4%)
  between operations  18.1 us (3%)
    psum x3, waiting for transfers between devices, head_total(): return lax.psum(partial_sum, 'head')  321 us
    unnamed x3, blocking collectives  107 us
    reduce_scatter x1, waiting for transfers between devices, on_device(): lax.psum_scatter(grad_w_fc_two, ('clip', 'seq'), scatter_dimension=1, til...  26 us
    unnamed x103, local copies, waits for them, and re-layouts  22.3 us
    all_gather x1, blocking collectives, fetch_weights(): lax.all_gather(w_key, ('clip', 'seq'), axis=0, tiled=True)  17.4 us
    all_gather x1, blocking collectives, fetch_weights(): lax.all_gather(w_out, ('clip', 'seq'), axis=1, tiled=True)  16.4 us
    all_gather x1, blocking collectives, fetch_weights(): lax.all_gather(w_value, ('clip', 'seq'), axis=0, tiled=True)  15.9 us
  transfers between devices with their start and end apart: 14, of which 5 were waited for; matrix products, arithmetic and copies ran while one was open for 11% of the time, Pallas kernels for 0%

profile of v1, /device:TPU:0, one launch (start us, length us, event | category | flops | bytes accessed | tf_op | source)
XLA Modules:
  0.0 709.3 jit_solution(6785153578488940923)
XLA Ops:
  8.1 3.1 collective-permute-start
  18.2 22.9 %all-reduce.17 = (bf16[768]{0:T(1024)(128)(2,1)S(1)}, bf16[768]{0:T(1024)(128)(2,1)S(1)}, bf16[768]{0:T(1024)(128)(2,1)S(1)}, bf16[768]{0:T(1024)(128)(2,1)S(1)}...) all-reduce(bf16[768]{0:T(1024)(128)(2,1)S(1)} %dynamic-update-slice, ...), channel_id=1, replica_groups=mesh['clip'=4,'seq'=2,'head'=4] {'clip','seq'}, use_global_device_ids=true, to_apply=%add.1 | all-reduce | flops 4608 | bytes 18432
  44.4 17.4 %all_gather.50 = bf16[768,192]{1,0:T(8,128)(2,1)S(1)} all-gather(bf16[96,192]{1,0:T(8,128)(2,1)S(1)} %copy-done.25), channel_id=1, replica_groups=mesh['clip'=4,'seq'=2,'head'=4] {'clip','seq'}, dimensions={0}, use_global_device_ids=true | all-gather | bytes 331776 | tf_op jit(solution)/shard_map/all_gather | solution.py:64
  61.8 15.9 %all_gather.48 = bf16[768,192]{1,0:T(8,128)(2,1)S(1)} all-gather(bf16[96,192]{1,0:T(8,128)(2,1)S(1)} %copy-done.26), channel_id=1, replica_groups=mesh['clip'=4,'seq'=2,'head'=4] {'clip','seq'}, dimensions={0}, use_global_device_ids=true | all-gather | bytes 331776 | tf_op jit(solution)/shard_map/all_gather | solution.py:65
  81.7 9.8 %all-gather.3 = bf16[2,750,192]{1,2,0:T(8,128)(2,1)S(1)} all-gather(bf16[1,750,192]{1,2,0:T(8,128)(2,1)} %fusion.39), channel_id=3, replica_groups=mesh['clip'=4,'seq'=2,'head'=4] {'seq'}, dimensions={0}, use_global_device_ids=true | all-gather | bytes 864000 | tf_op jit(solution)/shard_map/all_gather | solution.py:153
  96.9 8.5 %all-gather.2 = bf16[2,750,192]{1,2,0:T(8,128)(2,1)S(1)} all-gather(bf16[1,750,192]{1,2,0:T(8,128)(2,1)S(1)} %fusion.40), channel_id=2, replica_groups=mesh['clip'=4,'seq'=2,'head'=4] {'seq'}, dimensions={0}, use_global_device_ids=true | all-gather | bytes 864000 | tf_op jit(solution)/shard_map/all_gather | solution.py:154
  109.8 16.4 %all_gather.52 = bf16[192,768]{0,1:T(8,128)(2,1)S(1)} all-gather(bf16[192,96]{0,1:T(8,128)(2,1)S(1)} %copy.40), channel_id=1, replica_groups=mesh['clip'=4,'seq'=2,'head'=4] {'clip','seq'}, dimensions={1}, use_global_device_ids=true | all-gather | bytes 331776 | tf_op jit(solution)/shard_map/all_gather | solution.py:73
  128.1 7.0 multiply_reduce_fusion.1
  135.1 7.4 %fusion = f32[3,750]{1,0:T(4,128)S(1)} fusion(f32[3,750,1500]{2,1,0:T(8,128)} %get-tuple-element.151, f32[3,750]{1,0:T(4,128)S(1)} %get-tuple-element.150), kind=kLoop, calls=%fused_computation.5 | loop fusion | flops 10122750 | bytes 13518000 | tf_op jit(solution)/shard_map/while/body/eval_jaxpr/reduce_sum | solution.py:168
  142.5 6.6 fusion.38
  152.4 93.1 %all-reduce.23.cloned.1.call-done = f32[750,768]{1,0:T(8,128)} async-done(((f32[750,768]{1,0:T(8,128)}), f32[750,768]{1,0:T(8,128)}) %all-reduce.23.cloned.1.call-update) | async-done | bytes 2304016 | tf_op jit(solution)/shard_map/psum | solution.py:80
  248.0 8.9 %multiply_convert_fusion.1 = (bf16[750,768]{1,0:T(8,128)(2,1)}, f32[750,768]{1,0:T(8,128)}, f32[750,768]{1,0:T(8,128)}) fusion(f32[768]{0:T(1024)S(1)} %convert_element_type.151, bf16[768,768]{1,0:T(8,128)(2,1)} %all-gather.7.cloned.1.call-done, f32[750,768]{1,0:T(8,128)S(1)} %get-tuple-element.147, f32[768]{0:T(1024)S(1)} %convert_element_type.149, ...), kind=kOutput, calls=%fused_computation.48 | convolution fusion | flops 925632000 | bytes 9258864 | tf_op jit(solution)/shard_map/dot_general | solution.py:183
  256.9 4.8 convert_reduce_fusion.2
  267.1 4.2 fusion.73
  271.3 86.5 %all-reduce.25.cloned.1.call-done = f32[750,768]{1,0:T(8,128)} async-done(((f32[750,768]{1,0:T(8,128)}), f32[750,768]{1,0:T(8,128)}) %all-reduce.25.cloned.1.call-update) | async-done | bytes 2304016 | tf_op jit(solution)/shard_map/psum | solution.py:80
  363.3 12.2 %multiply_reduce_fusion = (f32[3,750]{1,0:T(4,128)S(1)}, f32[3,750,1500]{2,1,0:T(8,128)}) fusion(f32[3,750,1500]{2,1,0:T(8,128)} %get-tuple-element.151, f32[3,750]{1,0:T(4,128)S(1)} %log_add_fusion, bf16[750,3,64]{0,2,1:T(8,128)(2,1)S(1)} %bitcast.142, bf16[1500,3,64]{0,2,1:T(8,128)(2,1)S(1)} %copy-done.15), kind=kOutput, calls=%fused_computation.1 | convolution fusion | flops 445497760 | bytes 27882000 | tf_op jit(solution)/shard_map/while/body/eval_jaxpr/qhd,khd->hqk/dot_general | solution.py:268
  376.1 3.7 fusion.2
  381.3 10.1 %multiply_convert_fusion = bf16[3,750,1500]{2,1,0:T(8,128)(2,1)S(1)} fusion(f32[3,750,1500]{2,1,0:T(8,128)} %get-tuple-element.154, f32[3,750,1500]{2,1,0:T(8,128)} %get-tuple-element.151, f32[3,750]{1,0:T(4,128)S(1)} %get-tuple-element.153, f32[3,750]{1,0:T(4,128)S(1)} %log_add_fusion), kind=kLoop, calls=%fused_computation | loop fusion | flops 16875000 | bytes 33768000 | tf_op jit(solution)/shard_map/while/body/eval_jaxpr/convert_element_type | solution.py:272
  394.5 59.2 %all-reduce.28 = (bf16[1,1500,192]{1,2,0:T(8,128)(2,1)}, bf16[1,1500,192]{1,2,0:T(8,128)(2,1)}) all-reduce(f32[1,1500,192]{1,2,0:T(8,128)} %bitcast.141, f32[1,1500,192]{1,2,0:T(8,128)} %bitcast.140), channel_id=5, replica_groups=mesh['clip'=4,'seq'=2,'head'=4] {'seq'}, use_global_device_ids=true, to_apply=%region_13.14.clone | all-reduce | flops 576000 | bytes 3456000
  453.7 3.3 fusion.55
  460.0 5.5 convert_reduce_fusion.4
  466.2 3.2 add_add_fusion
  472.8 3.2 fusion.77
  476.0 2.9 fusion.53
  479.0 4.1 fusion.63
  483.2 4.2 fusion.43
  490.3 3.2 reduce-scatter.21.cloned.1.call-done
  495.1 141.8 %all-reduce.27.cloned.1.call-done = (f32[750,768]{1,0:T(8,128)}, f32[750,768]{1,0:T(8,128)}) async-done(((f32[750,768]{1,0:T(8,128)}, f32[750,768]{1,0:T(8,128)}), (f32[750,768]{1,0:T(8,128)}, f32[750,768]{1,0:T(8,128)})) %all-reduce.27.cloned.1.call-update) | async-done | bytes 4608016 | tf_op jit(solution)/shard_map/psum | solution.py:80
  639.6 24.7 %all-reduce.14 = (f32[768]{0:T(1024)S(1)}, f32[768]{0:T(1024)S(1)}, f32[192]{0:T(256)}, f32[192]{0:T(256)}, f32[768]{0:T(1024)S(1)}, /*index=5*/f32[768]{0:T(102...) all-reduce(f32[768]{0:T(1024)S(1)} %get-tuple-element.115, ...), channel_id=6, replica_groups=mesh['clip'=4,'seq'=2,'head'=4] {'clip','seq'}, use_global_device_ids=true, to_apply=%region_18.19.clone | all-reduce | flops 5760 | bytes 46080
  667.8 3.0 fusion.21
  670.8 3.8 copy.41
  676.0 26.0 %reduce-scatter.19.cloned.1.call-done = f32[768,96]{0,1:T(8,128)} async-done(((f32[768,768]{0,1:T(8,128)}), f32[768,96]{0,1:T(8,128)}) %reduce-scatter.19.cloned.1.call-update) | async-done | bytes 294928 | tf_op jit(solution)/shard_map/reduce_scatter | solution.py:338
  (182 shorter events, 64.6 us)
Async XLA Ops:
  8.0 69.7 %copy-start.1 = (bf16[1,750,768]{2,1,0:T(8,128)(2,1)S(1)}, bf16[1,750,768]{2,1,0:T(8,128)(2,1)}, u32[]{:S(2)}) copy-start(bf16[1,750,768]{2,1,0:T(8,128)(2,1)} %param.17) | copy-start | bytes 3456004
  8.0 36.3 %copy-start.25 = (bf16[96,192]{1,0:T(8,128)(2,1)S(1)}, bf16[96,192]{1,0:T(8,128)(2,1)}, u32[]{:S(2)}) copy-start(bf16[96,192]{1,0:T(8,128)(2,1)} %param.22) | copy-start | bytes 110596
  8.0 53.8 %copy-start.26 = (bf16[96,192]{1,0:T(8,128)(2,1)S(1)}, bf16[96,192]{1,0:T(8,128)(2,1)}, u32[]{:S(2)}) copy-start(bf16[96,192]{1,0:T(8,128)(2,1)} %param.23) | copy-start | bytes 110596
  8.1 69.7 %copy-start.32 = (bf16[192]{0:T(256)(128)(2,1)S(1)}, bf16[192]{0:T(256)(128)(2,1)}, u32[]{:S(2)}) copy-start(bf16[192]{0:T(256)(128)(2,1)} %param.24) | copy-start | bytes 1156
  8.1 237.5 %all-reduce.23.cloned.1.call-start = ((), (), s32[]{:S(2)}) async-start(), calls=%async_computation.6 | async-start | bytes 4620288 | tf_op jit(solution)/shard_map/psum | solution.py:80
  8.1 72.0 %collective-permute-start = (bf16[96,192]{1,0:T(8,128)(2,1)}, bf16[96,192]{1,0:T(8,128)(2,1)S(1)}, u32[]{:S(2)}, u32[]{:S(2)}) collective-permute-start(bf16[96,192]{1,0:T(8,128)(2,1)} %param.20), channel_id=1, source_target_pairs={{0,4},{4,0},{8,12},{12,8},{16,20},{20,16},{24,28},{28,24},{1,5},{5... | collective-permute-start | bytes 110600 | tf_op jit(solution)/shard_map/ppermute | solution.py:17
  61.8 18.3 %copy-start.9 = (bf16[768,192]{1,0:T(8,128)(2,1)}, bf16[768,192]{1,0:T(8,128)(2,1)S(1)}, u32[]{:S(2)}) copy-start(bf16[768,192]{1,0:T(8,128)(2,1)S(1)} %all_gather.50) | copy-start | bytes 884740
  80.2 15.0 %collective-permute-start.1 = (bf16[192,192]{1,0:T(8,128)(2,1)S(1)}, bf16[192,192]{1,0:T(8,128)(2,1)S(1)}, u32[]{:S(2)}, u32[]{:S(2)}) collective-permute-start(bf16[192,192]{1,0:T(8,128)(2,1)S(1)} %maximum_select_fusion.2), channel_id=1, source_target_pairs={{0,8},{4,12},{8,0},{12,4},{16,24},{20,28},{24,16},{28,20},{1,9},{5... | collective-permute-start | bytes 221192 | tf_op jit(solution)/shard_map/ppermute | solution.py:17
  93.0 16.7 %copy-start.27 = (bf16[192,96]{1,0:T(8,128)(2,1)S(1)}, bf16[192,96]{1,0:T(8,128)(2,1)}, u32[]{:S(2)}) copy-start(bf16[192,96]{1,0:T(8,128)(2,1)} %param.25) | copy-start | bytes 110596
  95.2 32.9 %copy-start.7 = (bf16[1500,3,64]{0,2,1:T(8,128)(2,1)}, bf16[1500,3,64]{0,2,1:T(8,128)(2,1)S(1)}, u32[]{:S(2)}) copy-start(bf16[1500,3,64]{0,2,1:T(8,128)(2,1)S(1)} %reshape.253) | copy-start | bytes 1728004
  96.1 30.0 %collective-permute-start.2 = (bf16[384,192]{1,0:T(8,128)(2,1)}, bf16[384,192]{1,0:T(8,128)(2,1)}, u32[]{:S(2)}, u32[]{:S(2)}) collective-permute-start(bf16[384,192]{1,0:T(8,128)(2,1)} %maximum_select_fusion.1), channel_id=1, source_target_pairs={{0,16},{4,20},{8,24},{12,28},{16,0},{20,4},{24,8},{28,12},{1,17},{... | collective-permute-start | bytes 442376 | tf_op jit(solution)/shard_map/ppermute | solution.py:17
  126.2 23.0 %copy-start.12 = (bf16[192,768]{0,1:T(8,128)(2,1)}, bf16[192,768]{0,1:T(8,128)(2,1)S(1)}, u32[]{:S(2)}) copy-start(bf16[192,768]{0,1:T(8,128)(2,1)S(1)} %all_gather.52) | copy-start | bytes 884740
  128.1 7.0 copy-start.20
  135.1 7.4 %copy-start.14 = (bf16[1500,3,64]{0,2,1:T(8,128)(2,1)S(1)}, bf16[1500,3,64]{0,2,1:T(8,128)(2,1)}, u32[]{:S(2)}) copy-start(bf16[1500,3,64]{0,2,1:T(8,128)(2,1)} %reshape.250) | copy-start | bytes 1728004
  151.1 96.9 %all-gather.7.cloned.1.call-start = ((), (), s32[]{:S(2)}) async-start(), calls=%async_computation.7 | async-start | bytes 1327104 | tf_op jit(solution)/shard_map/all_gather | solution.py:69
  151.7 105.2 %all-gather.9.cloned.1.call-start = ((), (), s32[]{:S(2)}) async-start(), calls=%async_computation.8 | async-start | bytes 1327104 | tf_op jit(solution)/shard_map/all_gather | solution.py:74
  152.3 205.5 %all-reduce.25.cloned.1.call-start = ((), (), s32[]{:S(2)}) async-start(), calls=%async_computation.9 | async-start | bytes 4620288 | tf_op jit(solution)/shard_map/psum | solution.py:80
  265.3 228.2 %reduce-scatter.21.cloned.1.call-start = ((), (), s32[]{:S(2)}) async-start(), calls=%async_computation.15 | async-start | bytes 884736
  361.8 18.1 %copy-start.2 = (f32[750,768]{1,0:T(8,128)}, f32[750,768]{1,0:T(8,128)S(1)}, u32[]{:S(2)}) copy-start(f32[750,768]{1,0:T(8,128)S(1)} %get-tuple-element.141) | copy-start | bytes 6912004
  361.8 13.7 %slice-start = ((s8[13860864]{0:T(1024)(128)(4,1)}), s8[4194304]{0:T(1024)(128)(4,1)S(1)}, s32[]{:S(2)}) async-start(s8[13860864]{0:T(1024)(128)(4,1)} %bitcast.138), calls=%async_computation.17 | async-start | bytes 8388608
  363.3 12.2 %slice-start.1 = ((s8[13860864]{0:T(1024)(128)(4,1)}), s8[4194304]{0:T(1024)(128)(4,1)S(1)}, s32[]{:S(2)}) async-start(s8[13860864]{0:T(1024)(128)(4,1)} %bitcast.138), calls=%async_computation.18 | async-start | bytes 8388608
  363.3 12.2 %slice-start.2 = ((s8[13860864]{0:T(1024)(128)(4,1)}), s8[4194304]{0:T(1024)(128)(4,1)S(1)}, s32[]{:S(2)}) async-start(s8[13860864]{0:T(1024)(128)(4,1)} %bitcast.138), calls=%async_computation.19 | async-start | bytes 8388608
  363.3 12.8 %slice-start.3 = ((s8[13860864]{0:T(1024)(128)(4,1)}), s8[1277952]{0:T(1024)(128)(4,1)S(1)}, s32[]{:S(2)}) async-start(s8[13860864]{0:T(1024)(128)(4,1)} %bitcast.138), calls=%async_computation.20 | async-start | bytes 2555904
  381.3 10.1 %copy-start.21 = (bf16[750,192]{0,1:T(8,128)(2,1)S(1)}, bf16[750,192]{0,1:T(8,128)(2,1)}, u32[]{:S(2)}) copy-start(bf16[750,192]{0,1:T(8,128)(2,1)} %copy-done.20) | copy-start | bytes 864004
  460.0 177.0 %all-reduce.27.cloned.1.call-start = ((), (), s32[]{:S(2)}) async-start(), calls=%async_computation.16 | async-start | bytes 9240576 | tf_op jit(solution)/shard_map/psum | solution.py:80
  460.0 6.2 copy-start.4
  460.0 6.2 copy-start.5
  469.5 206.5 %reduce-scatter.11.cloned.1.call-start = ((), (), s32[]{:S(2)}) async-start(), calls=%async_computation.10 | async-start | bytes 884736 | tf_op jit(solution)/shard_map/reduce_scatter | solution.py:327
  472.7 203.2 %reduce-scatter.15.cloned.1.call-start = ((), (), s32[]{:S(2)}) async-start(), calls=%async_computation.12 | async-start | bytes 884736 | tf_op jit(solution)/shard_map/reduce_scatter | solution.py:329
  475.9 200.0 %reduce-scatter.13.cloned.1.call-start = ((), (), s32[]{:S(2)}) async-start(), calls=%async_computation.11 | async-start | bytes 884736 | tf_op jit(solution)/shard_map/reduce_scatter | solution.py:328
  478.9 197.0 %reduce-scatter.17.cloned.1.call-start = ((), (), s32[]{:S(2)}) async-start(), calls=%async_computation.13 | async-start | bytes 2654208 | tf_op jit(solution)/shard_map/reduce_scatter | solution.py:333
  483.1 218.8 %reduce-scatter.19.cloned.1.call-start = ((), (), s32[]{:S(2)}) async-start(), calls=%async_computation.14 | async-start | bytes 2654208 | tf_op jit(solution)/shard_map/reduce_scatter | solution.py:338
  (22 other events, 50.1 us)
Sparse Core Ops, SparseCore 0:
  151.2 94.2 all-reduce.22
  265.4 92.3 all-reduce.24
  469.6 167.2 all-reduce.26
Sparse Core Ops, SparseCore 1:
  153.5 24.7 all-gather.6
  180.0 23.8 all-gather.8
  460.0 33.4 reduce-scatter.20
  497.2 34.9 reduce-scatter.10
  535.9 34.9 reduce-scatter.14
  574.6 34.8 reduce-scatter.12
  613.3 42.5 reduce-scatter.16
  659.6 42.2 reduce-scatter.18
